TPU v7x, 32 devices: a whole 2x2x4 slice. The times are simulated.
32 devices in a mesh: row: 8 (over y, x, core), col: 4 (over z).
Axes of the slice: x: 2, y: 2, z: 4, core: 2. Of those that a mesh axis runs over, the one named last changes fastest.
Arguments:
- weights: int32 [4096, 4096], P('row', 'col'), may hold values from 1 to 64
Outputs:
- distances: int32 [4096, 4096], P('row', 'col')
All inputs are finite; a program needn't handle non-finite values.
Results may differ from a plain program's by a relative error of at most 0.000001.
Values may be sent and summed in bfloat16 or wider, within the bound.
A program may use at most 64 MiB of HBM per device.

v0:
```python
import jax
import jax.numpy as jnp
from jax import lax
from jax.sharding import PartitionSpec as P

PIVOT = 128
STEPS = 4


def broadcast(value, axis, source):
    kept = jnp.where(lax.axis_index(axis) == source, value, 0).astype(value.dtype)
    return lax.psum(kept, axis)


def min_plus(acc, left, right):
    group = 8
    count = left.shape[1] // group

    def update(index, total):
        begin = (index * group).astype(jnp.int32)
        left_part = lax.dynamic_slice_in_dim(left, begin, group, 1)
        right_part = lax.dynamic_slice_in_dim(right, begin, group, 0)
        return jnp.minimum(total, jnp.min(left_part[:, :, None] + right_part[None, :, :], axis=1))

    return lax.fori_loop(0, count, update, acc)


def close_block(block):

    def relax(vertex, current):
        vertex = jnp.asarray(vertex).astype(jnp.int32)
        column = lax.dynamic_slice_in_dim(current, vertex, 1, 1)
        across = lax.dynamic_slice_in_dim(current, vertex, 1, 0)
        return jnp.minimum(current, column + across)

    return lax.fori_loop(0, block.shape[0], relax, block)


def per_device(weights):
    rows_dev, cols_dev = weights.shape
    verts = rows_dev * lax.axis_size("row")
    stride = verts // STEPS
    row_ids = lax.axis_index("row") * rows_dev + jnp.arange(rows_dev, dtype=jnp.int32)
    col_ids = lax.axis_index("col") * cols_dev + jnp.arange(cols_dev, dtype=jnp.int32)
    dist = jnp.where(row_ids[:, None] == col_ids[None, :], jnp.int32(0), weights).astype(jnp.int32)
    for step in range(STEPS):
        first = step * stride
        row_root = first // rows_dev
        row_off = first - row_root * rows_dev
        col_root = first // cols_dev
        col_off = first - col_root * cols_dev
        strip_rows = dist[row_off : row_off + PIVOT, :]
        strip_cols = dist[:, col_off : col_off + PIVOT]
        panel_rows = jax.tree.map(lambda part: broadcast(part, "row", row_root), strip_rows)
        closed = close_block(panel_rows[:, col_off : col_off + PIVOT])
        new_cols = min_plus(strip_cols, strip_cols, closed)
        panel_cols = jax.tree.map(lambda part: broadcast(part, "col", col_root), new_cols)
        dist = min_plus(dist, panel_cols, panel_rows)
    return dist


def solution(mesh):
    placed = (P("row", "col"),)
    return jax.shard_map(
        per_device, mesh=mesh, in_specs=placed, out_specs=P("row", "col"), check_vma=False
    )
```

profile of v0, /device:TPU:1, one launch (start us, length us, event | category | flops | bytes accessed | tf_op | source)
XLA Modules:
  0.0 1354.3 jit_solution(568644067238902018)
XLA Ops:
  9.3 57.0 %all-reduce.9.cloned.1.call-done = s32[128,1024]{1,0:T(8,128)} async-done(((s32[128,1024]{1,0:T(8,128)}), s32[128,1024]{1,0:T(8,128)}) %all-reduce.9.cloned.1.call-update) | async-done | bytes 524304 | tf_op jit(solution)/shard_map/psum | solution.py:12
  67.2 40.3 %while.156 = (s32[]{:T(128)}, s32[128,128]{1,0:T(8,128)S(1)}, s32[]{:T(128)}) while((s32[]{:T(128)}, s32[128,128]{1,0:T(8,128)S(1)}, s32[]{:T(128)}) %tuple.281), condition=%wide.region_2.3_spmd, body=%wide.region_1.2_spmd.sunk | while | flops 32770 | bytes 134197 | solution.py:36
  107.6 50.6 %while.157 = (s32[]{:T(128)}, s32[512,128]{1,0:T(8,128)S(1)}, s32[512,128]{1,0:T(8,128)S(1)}, s32[128,128]{1,0:T(8,128)S(1)}, s32[]{:T(128)}, /*index=5*/s32[]{:T(128)}, s32[]{:T(128)}, s32[]{:T(128)}) while((s32[]{:T(128)}, s32[512,128]{1,0:T(8,128)S(1)}, s32[512,128]{1,0:T(8,128)S(1)}, s32[128,128]{1,0:T(8,128)S(1)}, s32[]{:T(128)}, ...), condition=%wide.region_5.6_spmd, body=%wide.region_3.5_spmd.sunk | while | flops 1048582 | bytes 1110155 | solution.py:25
  159.0 33.7 %all-reduce.11.cloned.1.call-done = s32[512,128]{1,0:T(8,128)} async-done(((s32[512,128]{1,0:T(8,128)}), s32[512,128]{1,0:T(8,128)}) %all-reduce.11.cloned.1.call-update) | async-done | bytes 262160 | tf_op jit(solution)/shard_map/psum | solution.py:12
  192.7 150.9 %while.158 = (s32[]{:T(128)}, s32[512,1024]{1,0:T(8,128)S(1)}, s32[512,128]{1,0:T(8,128)}, s32[128,1024]{1,0:T(8,128)}, s32[]{:T(128)}, /*index=5*/s32[]{:T(128)}, s32[]{:T(128)}, s32[]{:T(128)}) while((s32[]{:T(128)}, s32[512,1024]{1,0:T(8,128)S(1)}, s32[512,128]{1,0:T(8,128)}, s32[128,1024]{1,0:T(8,128)}, s32[]{:T(128)}, ...), condition=%wide.region_9.10_spmd, body=%wide.region_7.9_spmd.sunk | while | flops 8388614 | bytes 8536203 | solution.py:25
  194.6 6.9 add_reduce_fusion.17
  204.0 6.9 add_reduce_fusion.17
  213.4 6.9 add_reduce_fusion.17
  222.9 6.9 add_reduce_fusion.17
  232.3 6.9 add_reduce_fusion.17
  241.7 6.9 add_reduce_fusion.17
  251.2 6.9 add_reduce_fusion.17
  260.6 6.9 add_reduce_fusion.17
  270.0 6.9 add_reduce_fusion.17
  279.5 6.9 add_reduce_fusion.17
  288.9 6.9 add_reduce_fusion.17
  298.3 6.9 add_reduce_fusion.17
  307.8 6.9 add_reduce_fusion.17
  317.2 6.9 add_reduce_fusion.17
  326.6 6.9 add_reduce_fusion.17
  336.1 6.9 add_reduce_fusion.17
  344.6 55.9 %all-reduce.13.cloned.1.call-done = s32[128,1024]{1,0:T(8,128)} async-done(((s32[128,1024]{1,0:T(8,128)}), s32[128,1024]{1,0:T(8,128)}) %all-reduce.13.cloned.1.call-update) | async-done | bytes 524304 | tf_op jit(solution)/shard_map/psum | solution.py:12
  401.4 40.3 %while.159 = (s32[]{:T(128)}, s32[128,128]{1,0:T(8,128)S(1)}, s32[]{:T(128)}) while((s32[]{:T(128)}, s32[128,128]{1,0:T(8,128)S(1)}, s32[]{:T(128)}) %tuple.290), condition=%wide.region_12.13_spmd, body=%wide.region_11.12_spmd.sunk | while | flops 32770 | bytes 134197 | solution.py:36
  441.7 50.6 %while.160 = (s32[]{:T(128)}, s32[512,128]{1,0:T(8,128)S(1)}, s32[512,128]{1,0:T(8,128)S(1)}, s32[128,128]{1,0:T(8,128)S(1)}, s32[]{:T(128)}, /*index=5*/s32[]{:T(128)}, s32[]{:T(128)}, s32[]{:T(128)}) while((s32[]{:T(128)}, s32[512,128]{1,0:T(8,128)S(1)}, s32[512,128]{1,0:T(8,128)S(1)}, s32[128,128]{1,0:T(8,128)S(1)}, s32[]{:T(128)}, ...), condition=%wide.region_15.16_spmd, body=%wide.region_13.15_spmd.sunk | while | flops 1048582 | bytes 1110155 | solution.py:25
  493.2 33.7 %all-reduce.15.cloned.1.call-done = s32[512,128]{1,0:T(8,128)} async-done(((s32[512,128]{1,0:T(8,128)}), s32[512,128]{1,0:T(8,128)}) %all-reduce.15.cloned.1.call-update) | async-done | bytes 262160 | tf_op jit(solution)/shard_map/psum | solution.py:12
  526.9 150.9 %while.161 = (s32[]{:T(128)}, s32[512,1024]{1,0:T(8,128)S(1)}, s32[512,128]{1,0:T(8,128)}, s32[128,1024]{1,0:T(8,128)}, s32[]{:T(128)}, /*index=5*/s32[]{:T(128)}, s32[]{:T(128)}, s32[]{:T(128)}) while((s32[]{:T(128)}, s32[512,1024]{1,0:T(8,128)S(1)}, s32[512,128]{1,0:T(8,128)}, s32[128,1024]{1,0:T(8,128)}, s32[]{:T(128)}, ...), condition=%wide.region_19.20_spmd, body=%wide.region_17.19_spmd.sunk | while | flops 8388614 | bytes 8536203 | solution.py:25
  528.7 6.9 add_reduce_fusion.19
  538.2 6.9 add_reduce_fusion.19
  547.6 6.9 add_reduce_fusion.19
  557.0 6.9 add_reduce_fusion.19
  566.5 6.9 add_reduce_fusion.19
  575.9 6.9 add_reduce_fusion.19
  585.3 6.9 add_reduce_fusion.19
  594.8 6.9 add_reduce_fusion.19
  604.2 6.9 add_reduce_fusion.19
  613.6 6.9 add_reduce_fusion.19
  623.1 6.9 add_reduce_fusion.19
  632.5 6.9 add_reduce_fusion.19
  641.9 6.9 add_reduce_fusion.19
  651.4 6.9 add_reduce_fusion.19
  660.8 6.9 add_reduce_fusion.19
  670.2 6.9 add_reduce_fusion.19
  678.8 55.9 %all-reduce.17.cloned.1.call-done = s32[128,1024]{1,0:T(8,128)} async-done(((s32[128,1024]{1,0:T(8,128)}), s32[128,1024]{1,0:T(8,128)}) %all-reduce.17.cloned.1.call-update) | async-done | bytes 524304 | tf_op jit(solution)/shard_map/psum | solution.py:12
  735.5 40.3 %while.162 = (s32[]{:T(128)}, s32[128,128]{1,0:T(8,128)S(1)}, s32[]{:T(128)}) while((s32[]{:T(128)}, s32[128,128]{1,0:T(8,128)S(1)}, s32[]{:T(128)}) %tuple.299), condition=%wide.region_22.23_spmd, body=%wide.region_21.22_spmd.sunk | while | flops 32770 | bytes 134197 | solution.py:36
  775.9 50.6 %while.163 = (s32[]{:T(128)}, s32[512,128]{1,0:T(8,128)S(1)}, s32[512,128]{1,0:T(8,128)S(1)}, s32[128,128]{1,0:T(8,128)S(1)}, s32[]{:T(128)}, /*index=5*/s32[]{:T(128)}, s32[]{:T(128)}, s32[]{:T(128)}) while((s32[]{:T(128)}, s32[512,128]{1,0:T(8,128)S(1)}, s32[512,128]{1,0:T(8,128)S(1)}, s32[128,128]{1,0:T(8,128)S(1)}, s32[]{:T(128)}, ...), condition=%wide.region_25.26_spmd, body=%wide.region_23.25_spmd.sunk | while | flops 1048582 | bytes 1110155 | solution.py:25
  827.5 33.6 %all-reduce.19.cloned.1.call-done = s32[512,128]{1,0:T(8,128)} async-done(((s32[512,128]{1,0:T(8,128)}), s32[512,128]{1,0:T(8,128)}) %all-reduce.19.cloned.1.call-update) | async-done | bytes 262160 | tf_op jit(solution)/shard_map/psum | solution.py:12
  861.1 150.9 %while.164 = (s32[]{:T(128)}, s32[512,1024]{1,0:T(8,128)S(1)}, s32[512,128]{1,0:T(8,128)}, s32[128,1024]{1,0:T(8,128)}, s32[]{:T(128)}, /*index=5*/s32[]{:T(128)}, s32[]{:T(128)}, s32[]{:T(128)}) while((s32[]{:T(128)}, s32[512,1024]{1,0:T(8,128)S(1)}, s32[512,128]{1,0:T(8,128)}, s32[128,1024]{1,0:T(8,128)}, s32[]{:T(128)}, ...), condition=%wide.region_29.30_spmd, body=%wide.region_27.29_spmd.sunk | while | flops 8388614 | bytes 8536203 | solution.py:25
  862.9 6.9 add_reduce_fusion.21
  872.3 6.9 add_reduce_fusion.21
  881.8 6.9 add_reduce_fusion.21
  891.2 6.9 add_reduce_fusion.21
  900.6 6.9 add_reduce_fusion.21
  910.1 6.9 add_reduce_fusion.21
  919.5 6.9 add_reduce_fusion.21
  928.9 6.9 add_reduce_fusion.21
  938.4 6.9 add_reduce_fusion.21
  1012.9 55.9 %all-reduce.21.cloned.1.call-done = s32[128,1024]{1,0:T(8,128)} async-done(((s32[128,1024]{1,0:T(8,128)}), s32[128,1024]{1,0:T(8,128)}) %all-reduce.21.cloned.1.call-update) | async-done | bytes 524304 | tf_op jit(solution)/shard_map/psum | solution.py:12
  1069.7 40.3 %while.165 = (s32[]{:T(128)}, s32[128,128]{1,0:T(8,128)S(1)}, s32[]{:T(128)}) while((s32[]{:T(128)}, s32[128,128]{1,0:T(8,128)S(1)}, s32[]{:T(128)}) %tuple.308), condition=%wide.region_32.33_spmd, body=%wide.region_31.32_spmd.sunk | while | flops 32770 | bytes 134197 | solution.py:36
  1110.0 50.6 %while.166 = (s32[]{:T(128)}, s32[512,128]{1,0:T(8,128)S(1)}, s32[512,128]{1,0:T(8,128)S(1)}, s32[128,128]{1,0:T(8,128)S(1)}, s32[]{:T(128)}, /*index=5*/s32[]{:T(128)}, s32[]{:T(128)}, s32[]{:T(128)}) while((s32[]{:T(128)}, s32[512,128]{1,0:T(8,128)S(1)}, s32[512,128]{1,0:T(8,128)S(1)}, s32[128,128]{1,0:T(8,128)S(1)}, s32[]{:T(128)}, ...), condition=%wide.region_35.36_spmd, body=%wide.region_33.35_spmd.sunk | while | flops 1048582 | bytes 1110155 | solution.py:25
  1161.4 33.8 %all-reduce.23.cloned.1.call-done = s32[512,128]{1,0:T(8,128)} async-done(((s32[512,128]{1,0:T(8,128)}), s32[512,128]{1,0:T(8,128)}) %all-reduce.23.cloned.1.call-update) | async-done | bytes 262160 | tf_op jit(solution)/shard_map/psum | solution.py:12
  1195.2 150.9 %while.167 = (s32[]{:T(128)}, s32[512,1024]{1,0:T(8,128)S(1)}, s32[512,128]{1,0:T(8,128)}, s32[128,1024]{1,0:T(8,128)}, s32[]{:T(128)}, /*index=5*/s32[]{:T(128)}, s32[]{:T(128)}, s32[]{:T(128)}) while((s32[]{:T(128)}, s32[512,1024]{1,0:T(8,128)S(1)}, s32[512,128]{1,0:T(8,128)}, s32[128,1024]{1,0:T(8,128)}, s32[]{:T(128)}, ...), condition=%wide.region_39.40_spmd, body=%wide.region_37.39_spmd.sunk | while | flops 8388614 | bytes 8536203 | solution.py:25
  1197.1 6.9 add_reduce_fusion.23
  1206.5 6.9 add_reduce_fusion.23
  1215.9 6.9 add_reduce_fusion.23
  (2045 shorter events, 653.4 us)
Async XLA Ops:
  6.5 59.8 %all-reduce.9.cloned.1.call-start = ((), (), s32[]{:S(2)}) async-start(), calls=%async_computation | async-start | bytes 1048576 | tf_op jit(solution)/shard_map/psum | solution.py:12
  9.2 183.5 %all-reduce.11.cloned.1.call-start = ((), (), s32[]{:S(2)}) async-start(), calls=%async_computation.1 | async-start | bytes 524288 | tf_op jit(solution)/shard_map/psum | solution.py:12
  158.9 241.6 %all-reduce.13.cloned.1.call-start = ((), (), s32[]{:S(2)}) async-start(), calls=%async_computation.2 | async-start | bytes 1048576 | tf_op jit(solution)/shard_map/psum | solution.py:12
  344.5 182.4 %all-reduce.15.cloned.1.call-start = ((), (), s32[]{:S(2)}) async-start(), calls=%async_computation.3 | async-start | bytes 524288 | tf_op jit(solution)/shard_map/psum | solution.py:12
  493.1 241.6 %all-reduce.17.cloned.1.call-start = ((), (), s32[]{:S(2)}) async-start(), calls=%async_computation.4 | async-start | bytes 1048576 | tf_op jit(solution)/shard_map/psum | solution.py:12
  678.7 182.4 %all-reduce.19.cloned.1.call-start = ((), (), s32[]{:S(2)}) async-start(), calls=%async_computation.5 | async-start | bytes 524288 | tf_op jit(solution)/shard_map/psum | solution.py:12
  827.3 241.6 %all-reduce.21.cloned.1.call-start = ((), (), s32[]{:S(2)}) async-start(), calls=%async_computation.6 | async-start | bytes 1048576 | tf_op jit(solution)/shard_map/psum | solution.py:12
  1012.8 182.4 %all-reduce.23.cloned.1.call-start = ((), (), s32[]{:S(2)}) async-start(), calls=%async_computation.7 | async-start | bytes 524288 | tf_op jit(solution)/shard_map/psum | solution.py:12
  1346.1 1.3 copy-start
Sparse Core Ops, SparseCore 0:
  10.4 55.9 all-reduce.8
  159.1 33.6 all-reduce.10
  344.6 55.8 all-reduce.12
  493.2 33.6 all-reduce.14
  678.8 55.8 all-reduce.16
  827.4 33.6 all-reduce.18
  1012.9 55.8 all-reduce.20
  1161.5 33.6 all-reduce.22
where the time goes:
time: 1360 us; the launch traced here: 1350 us
  other arithmetic  730 us (54%)
  waiting for transfers between devices  360 us (26%)
  local copies, waits for them, and re-layouts  226 us (17%)
  loops' own time  23.8 us (2%)
  between operations  13.7 us (1%)
    reduce_min x128, other arithmetic, update(): jnp.min(left_part[:, :, None] + right_part[None, :, :], axis=1)  628 us
    psum x8, waiting for transfers between devices, broadcast(): return lax.psum(kept, axis)  360 us
    dynamic_slice x512, local copies, waits for them, and re-layouts, relax(): column = lax.dynamic_slice_in_dim(current, vertex, 1, 1)  89.7 us
    dynamic_slice x128, local copies, waits for them, and re-layouts, update(): left_part = lax.dynamic_slice_in_dim(left, begin, group, 1)  77 us
    dynamic_slice x128, local copies, waits for them, and re-layouts, update(): right_part = lax.dynamic_slice_in_dim(right, begin, group, 0)  49.8 us
    min x512, other arithmetic, relax(): return jnp.minimum(current, column + across)  49 us
    min x128, other arithmetic, update(): jnp.minimum(total, jnp.min(left_part[:, :, None] + right_part[None, :, :]...  45.4 us
  transfers between devices with their start and end apart: 8, of which 8 were waited for; matrix products, arithmetic and copies ran while one was open for 0% of the time, Pallas kernels for 0%

commit v1 on v0

v1 whole, which is shorter than its diff:
```python
import jax
import jax.numpy as jnp
from jax import lax
from jax.experimental import pallas as pl
from jax.experimental.pallas import tpu as pltpu
from jax.sharding import PartitionSpec as P

PIVOT = 128
STEPS = 4
MESH = pl.DeviceIdType.MESH

BETA = 7.03
SLACK = 0.0021
LOW_LEFT = ((18.09, 0, 36), (0.10, 0, 17))
LOW_RIGHT = ((0.10, 0, 17), (18.09, 18, 36))
LOW_SUM = 18.19
HIGH_LEFT = ((18.09, 0, 36), (35.09, 17, 36), (8.09, 0, 26), (45.09, 37, 63))
HIGH_RIGHT = ((35.09, 17, 53), (18.09, 0, 16), (45.09, 54, 63), (8.09, 0, 26))
HIGH_SUM = 53.18
HIGH_FIRST = 36.0


def window(dist, centre, first, last):
    power = jnp.exp2((centre - dist) * BETA)
    kept = dist <= last if first == 0 else (dist >= first) & (dist <= last)
    return jnp.where(kept, power, 0.0).astype(jnp.bfloat16)


def encode(dist, windows, axis):
    return jnp.concatenate([window(dist, *part) for part in windows], axis=axis)


def encode_left(dist):
    return encode(dist, LOW_LEFT, 1), encode(dist, HIGH_LEFT, 1)


def encode_right(dist):
    return encode(dist, LOW_RIGHT, 0), encode(dist, HIGH_RIGHT, 0)


def product(left, right):
    return jnp.dot(left, right, preferred_element_type=jnp.float32)


def decode(low, high):
    low = (LOW_SUM - SLACK) - jnp.log2(low) * (1.0 / BETA)
    high = (HIGH_SUM - SLACK) - jnp.log2(high) * (1.0 / BETA)
    return jnp.ceil(jnp.minimum(low, jnp.maximum(high, HIGH_FIRST)))


def min_plus(left, right):
    return decode(product(left[0], right[0]), product(left[1], right[1]))


def gather_kernel(n_row, n_col, strip_rows, strip_cols, panel_rows, panel_cols, pivots,
                  send_rows, recv_rows, send_cols, recv_cols, send_piv, recv_piv, local_sem):
    r, c = lax.axis_index("row"), lax.axis_index("col")
    row_gap, col_gap = n_row // STEPS, n_col // STEPS
    barrier = pltpu.get_barrier_semaphore()
    for k in range(1, n_row):
        pl.semaphore_signal(barrier, inc=1, device_id=(lax.rem(r + k, n_row), c), device_id_type=MESH)
    for k in range(1, n_col):
        pl.semaphore_signal(barrier, inc=1, device_id=(r, lax.rem(c + k, n_col)), device_id_type=MESH)
    pl.semaphore_wait(barrier, n_row + n_col - 2)

    def cols_copy(s, k):
        return pltpu.make_async_remote_copy(
            src_ref=strip_cols, dst_ref=panel_cols.at[s],
            send_sem=send_cols.at[k - 1], recv_sem=recv_cols.at[s],
            device_id=(r, lax.rem(c + k, n_col)), device_id_type=MESH)

    def rows_copy(s, k):
        return pltpu.make_async_remote_copy(
            src_ref=strip_rows, dst_ref=panel_rows.at[s],
            send_sem=send_rows.at[k - 1], recv_sem=recv_rows.at[s],
            device_id=(lax.rem(r + k, n_row), c), device_id_type=MESH)

    def piv_copy(s, k):
        return pltpu.make_async_remote_copy(
            src_ref=panel_cols.at[:, pl.ds(0, PIVOT)], dst_ref=pivots.at[s],
            send_sem=send_piv.at[k - 1], recv_sem=recv_piv.at[s],
            device_id=(lax.rem(r + k, n_row), c), device_id_type=MESH)

    for s in range(STEPS):
        @pl.when(c == s * col_gap)
        def _():
            for k in range(1, n_col):
                cols_copy(s, k).start()
            own = pltpu.make_async_copy(strip_cols, panel_cols.at[s], local_sem.at[0])
            own.start()
            own.wait()

    for s in range(STEPS):
        @pl.when(r == s * row_gap)
        def _():
            for k in range(1, n_row):
                rows_copy(s, k).start()
            own = pltpu.make_async_copy(strip_rows, panel_rows.at[s], local_sem.at[1])
            own.start()
            own.wait()

    for s in range(STEPS):
        @pl.when(c != s * col_gap)
        def _():
            cols_copy(s, 1).wait_recv()

    for s in range(STEPS):
        @pl.when(r == s * row_gap)
        def _():
            for k in range(1, n_row):
                piv_copy(s, k).start()
            own = pltpu.make_async_copy(panel_cols.at[:, pl.ds(0, PIVOT)], pivots.at[s], local_sem.at[2])
            own.start()
            own.wait()

    for s in range(STEPS):
        @pl.when(r != s * row_gap)
        def _():
            rows_copy(s, 1).wait_recv()
            piv_copy(s, 1).wait_recv()

    for s in range(STEPS):
        @pl.when(c == s * col_gap)
        def _():
            for k in range(1, n_col):
                cols_copy(s, k).wait_send()

        @pl.when(r == s * row_gap)
        def _():
            for k in range(1, n_row):
                rows_copy(s, k).wait_send()
                piv_copy(s, k).wait_send()


def gather(n_row, n_col, strip_rows, strip_cols):
    rows_dev, cols_dev = strip_cols.shape[0], strip_rows.shape[1]
    vmem = pl.BlockSpec(memory_space=pltpu.VMEM)
    dma = pltpu.SemaphoreType.DMA
    return pl.pallas_call(
        lambda *refs: gather_kernel(n_row, n_col, *refs),
        out_shape=(
            jax.ShapeDtypeStruct((STEPS, PIVOT, cols_dev), jnp.bfloat16),
            jax.ShapeDtypeStruct((STEPS, rows_dev, PIVOT), jnp.bfloat16),
            jax.ShapeDtypeStruct((STEPS, STEPS, PIVOT, PIVOT), jnp.bfloat16),
        ),
        in_specs=[vmem] * 2,
        out_specs=(vmem,) * 3,
        scratch_shapes=[
            dma((n_row - 1,)), dma((STEPS,)), dma((n_col - 1,)), dma((STEPS,)),
            dma((n_row - 1,)), dma((STEPS,)), dma((3,)),
        ],
        compiler_params=pltpu.CompilerParams(collective_id=0, has_side_effects=True),
    )(strip_rows, strip_cols)


def close_block(block):
    def more(state):
        return (state[0] < 6) & state[1]

    def square(state):
        count, _, now = state
        new = jnp.minimum(now, min_plus(encode_left(now), encode_right(now)))
        return count + 1, jnp.max(now - new) > 0.5, new

    return lax.while_loop(more, square, (jnp.int32(0), jnp.bool_(True), block))[2]


def close_kernel(panel_cols, pivots, closed, dist):
    size = STEPS * PIVOT
    rows = panel_cols.shape[1]
    tile = 256
    for s in range(STEPS):
        for t in range(STEPS):
            dist[s * PIVOT : (s + 1) * PIVOT, t * PIVOT : (t + 1) * PIVOT] = pivots[s, t].astype(jnp.float32)
        dist[size : size + rows, s * PIVOT : (s + 1) * PIVOT] = panel_cols[s].astype(jnp.float32)
    for s in range(STEPS):
        mine = slice(s * PIVOT, (s + 1) * PIVOT)
        block = close_block(dist[mine, mine])
        block_right = encode_right(block)
        across_right = encode_right(dist[mine, :])

        def update(index, carry):
            part = pl.ds(pl.multiple_of(index * tile, tile), tile)
            column = min_plus(encode_left(dist[part, mine]), block_right)
            dist[part, :] = jnp.minimum(dist[part, :], min_plus(encode_left(column), across_right))
            return carry

        lax.fori_loop(0, (size + rows) // tile, update, 0)
    for s in range(STEPS):
        closed[s] = dist[size : size + rows, s * PIVOT : (s + 1) * PIVOT].astype(jnp.bfloat16)


def close(panel_cols, pivots):
    rows = panel_cols.shape[1]
    vmem = pl.BlockSpec(memory_space=pltpu.VMEM)
    return pl.pallas_call(
        close_kernel,
        out_shape=jax.ShapeDtypeStruct(panel_cols.shape, jnp.bfloat16),
        in_specs=[vmem] * 2,
        out_specs=vmem,
        scratch_shapes=[pltpu.VMEM((STEPS * PIVOT + rows, STEPS * PIVOT), jnp.float32)],
    )(panel_cols, pivots)


def finish_kernel(offset, closed, panel_rows, weights, out, low_right, high_right, low_left, high_left):
    tile, cols = weights.shape
    wide = 256

    @pl.when(pl.program_id(0) == 0)
    def _():
        def one(index, carry):
            s, part = index // (cols // wide), index % (cols // wide)
            where = pl.ds(pl.multiple_of(part * wide, wide), wide)
            low, high = encode_right(panel_rows[s, :, where].astype(jnp.float32))
            low_right[s, :, where] = low
            high_right[s, :, where] = high
            return carry

        lax.fori_loop(0, STEPS * (cols // wide), one, 0)

    for s in range(STEPS):
        low, high = encode_left(closed[s].astype(jnp.float32))
        low_left[s] = low
        high_left[s] = high

    base = offset[0] + pl.program_id(0) * tile

    def columns(index, carry):
        start = pl.multiple_of(index * wide, wide)
        where = pl.ds(start, wide)
        low = product(low_left[0], low_right[0, :, where])
        high = product(high_left[0], high_right[0, :, where])
        for s in range(1, STEPS):
            low = jnp.maximum(low, product(low_left[s], low_right[s, :, where]))
            high = jnp.maximum(high, product(high_left[s], high_right[s, :, where]))
        shape = (tile, wide)
        gap = lax.broadcasted_iota(jnp.int32, shape, 0) - lax.broadcasted_iota(jnp.int32, shape, 1)
        old = jnp.where(gap == start - base, 0, weights[:, where])
        best = jnp.minimum(decode(low, high), 64.0).astype(jnp.int32)
        out[:, where] = jnp.minimum(old, best)
        return carry

    lax.fori_loop(0, cols // wide, columns, 0)


def finish(offset, closed, panel_rows, weights):
    rows, cols = weights.shape
    tile = 256
    return pl.pallas_call(
        finish_kernel,
        out_shape=jax.ShapeDtypeStruct(weights.shape, jnp.int32),
        grid=(rows // tile,),
        in_specs=[
            pl.BlockSpec(memory_space=pltpu.SMEM),
            pl.BlockSpec((STEPS, tile, PIVOT), lambda i: (0, i, 0)),
            pl.BlockSpec((STEPS, PIVOT, cols), lambda i: (0, 0, 0)),
            pl.BlockSpec((tile, cols), lambda i: (i, 0)),
        ],
        out_specs=pl.BlockSpec((tile, cols), lambda i: (i, 0)),
        scratch_shapes=[
            pltpu.VMEM((STEPS, 2 * PIVOT, cols), jnp.bfloat16),
            pltpu.VMEM((STEPS, 4 * PIVOT, cols), jnp.bfloat16),
            pltpu.VMEM((STEPS, tile, 2 * PIVOT), jnp.bfloat16),
            pltpu.VMEM((STEPS, tile, 4 * PIVOT), jnp.bfloat16),
        ],
    )(offset, closed, panel_rows, weights)


def solution(mesh):
    n_row, n_col = mesh.shape["row"], mesh.shape["col"]
    assert n_row % STEPS == 0 and n_col % STEPS == 0

    def per_device(weights):
        rows_dev, cols_dev = weights.shape
        offset = lax.axis_index("row") * rows_dev - lax.axis_index("col") * cols_dev
        down = jnp.arange(rows_dev, dtype=jnp.int32)[:, None] + offset
        across = jnp.arange(cols_dev, dtype=jnp.int32)[None, :]

        def strip(height, width):
            kept = weights[:height, :width]
            return jnp.where(down[:height] == across[:, :width], 0, kept).astype(jnp.bfloat16)

        panel_rows, panel_cols, pivots = gather(
            n_row, n_col, strip(PIVOT, cols_dev), strip(rows_dev, PIVOT))
        closed = close(panel_cols, pivots)
        return finish(jnp.full((1,), offset, jnp.int32), closed, panel_rows, weights)

    return jax.shard_map(
        per_device, mesh=mesh, in_specs=(P("row", "col"),), out_specs=P("row", "col"), check_vma=False)
```

time: 1360 us -> 65.3 us (0.05)
  other arithmetic: 730 us -> 3.65 us
  waiting for transfers between devices: 360 us -> 0 us
  local copies, waits for them, and re-layouts: 226 us -> 0 us
  Pallas kernels: 0 us -> 61.4 us
  loops' own time: 23.8 us -> 0 us
  between operations: 13.7 us -> 0.02 us
    reduce_min x128 -> x0, other arithmetic: 628 us -> none  [update(): jnp.min(left_part[:, :, None] + right_part[None, :, :], axis=1)]
    psum x8 -> x0, waiting for transfers between devices: 360 us -> none  [broadcast(): return lax.psum(kept, axis)]
    dynamic_slice x768 -> x0, local copies, waits for them, and re-layouts: 217 us -> none  [the longest x512 89.7 us: relax(): column = lax.dynamic_slice_in_dim(current, vertex, 1, 1)]
    min x640 -> x0, other arithmetic: 94.4 us -> none  [the longest x512 49 us: relax(): return jnp.minimum(current, column + across)]
    pallas_call x0 -> x3, Pallas kernels: none -> 61.4 us  [the longest x1 27.2 us: gather(): pl.pallas_call(lambda *refs: gather_kernel(n_row, n_col, *refs), out_shap...]
    another operation x12 -> x0, loops' own time: 23.8 us -> none  [the longest x4 17.7 us: close_block(): return lax.fori_loop(0, block.shape[0], relax, block)]
  transfers between devices with their start and end apart: 8 -> 0, of which waited for: 8 -> 0; matrix products, arithmetic and copies ran while one was open for 0% -> 0% of each run, Pallas kernels for 0% -> 0%
where the time goes in v1:
time: 65.3 us; the launch traced here: 65 us
  Pallas kernels  61.4 us (94%)
  other arithmetic  3.65 us (6%)
    pallas_call x1, Pallas kernels, gather(): pl.pallas_call(lambda *refs: gather_kernel(n_row, n_col, *refs), out_shap...  27.2 us
    pallas_call x1, Pallas kernels, close(): pl.pallas_call(close_kernel, out_shape=jax.ShapeDtypeStruct(panel_cols.sh...  22.2 us
    pallas_call x1, Pallas kernels, finish(): pl.pallas_call(finish_kernel, out_shape=jax.ShapeDtypeStruct(weights.shap...  12 us
    convert_element_type x2, other arithmetic, strip(): jnp.where(down[:height] == across[:, :width], 0, kept).astype(jnp.bfloat16)  3.64 us

profile of v1, /device:TPU:1, one launch (start us, length us, event | category | flops | bytes accessed | tf_op | source)
XLA Modules:
  0.0 65.0 jit_solution(8583684531476238329)
XLA Ops:
  0.0 1.8 %select_convert_fusion.1.refs_1_ = bf16[512,128]{1,0:T(8,128)(2,1)} fusion(s32[512,1024]{1,0:T(8,128)} %weights.1, s32[128]{0:T(128)S(1)} %add_bitcast_fusion, s32[512]{0:T(512)S(1)} %iota_add_fusion), kind=kLoop, calls=%fused_computation.2 | loop fusion | flops 196608 | bytes 395776 | tf_op jit(solution)/shard_map/convert_element_type | solution.py:281
  1.8 1.9 %select_convert_fusion.refs_0_ = bf16[128,1024]{1,0:T(8,128)(2,1)} fusion(s32[512,1024]{1,0:T(8,128)} %weights.1, s32[128]{0:T(128)S(1)} %fusion), kind=kLoop, calls=%fused_computation | loop fusion | flops 393216 | bytes 786944 | tf_op jit(solution)/shard_map/convert_element_type | solution.py:281
  3.7 27.2 %shard_map.17 = (bf16[4,128,1024]{2,1,0:T(8,128)(2,1)}, bf16[4,512,128]{2,1,0:T(8,128)(2,1)}, bf16[4,4,128,128]{3,2,1,0:T(8,128)(2,1)}) custom-call(bf16[128,1024]{1,0:T(8,128)(2,1)} %select_convert_fusion.refs_0_, bf16[512,128]{1,0:T(8,128)(2,1)} %select_convert_fusion.1.refs_1_), custom_call_target="tpu_custom_call" | custom-call | tf_op jit(solution)/shard_map/pallas_call | solution.py:139
  30.8 22.2 %shard_map.18.closed = bf16[4,512,128]{2,1,0:T(8,128)(2,1)} custom-call(bf16[4,512,128]{2,1,0:T(8,128)(2,1)} %get-tuple-element.8.panel_cols, bf16[4,4,128,128]{3,2,1,0:T(8,128)(2,1)} %get-tuple-element.9.pivots), custom_call_target="tpu_custom_call" | custom-call | tf_op jit(solution)/shard_map/pallas_call | solution.py:196
  53.0 12.0 %shard_map.19 = s32[512,1024]{1,0:T(8,128)} custom-call(s32[1]{0:T(128)} %bitcast.offset, bf16[4,512,128]{2,1,0:T(8,128)(2,1)} %shard_map.18.closed, bf16[4,128,1024]{2,1,0:T(8,128)(2,1)} %get-tuple-element.10.panel_rows, s32[512,1024]{1,0:T(8,128)} %weights.1), custom_call_target="tpu_custom_call" | custom-call | tf_op jit(solution)/shard_map/pallas_call | solution.py:249
  (3 shorter events, 0.0 us)

commit v2 on v1

v2 whole, which is shorter than its diff:
```python
import jax
import jax.numpy as jnp
from jax import lax
from jax.experimental import pallas as pl
from jax.experimental.pallas import tpu as pltpu
from jax.sharding import PartitionSpec as P

PIVOT = 128
STEPS = 4
MESH = pl.DeviceIdType.MESH

BETA = 7.03
SLACK = 0.0021
LOW_SUM = 18.19
HIGH_LEFT = ((18.09, 0, 36), (35.09, 17, 36), (8.09, 0, 26), (45.09, 37, 63))
HIGH_RIGHT = ((35.09, 17, 53), (18.09, 0, 16), (45.09, 54, 63), (8.09, 0, 26))
HIGH_SUM = 53.18
HIGH_FIRST = 36.0


def step_of(centre, base):
    return 2.0 ** (BETA * (centre - base))


def power(scaled, centre):
    return jnp.exp2(BETA * centre - scaled)


def keep(value, dist, first, last):
    kept = dist <= last if first == 0 else (dist >= first) & (dist <= last)
    return jnp.where(kept, value, 0.0).astype(jnp.bfloat16)


def encode_left(dist):
    scaled = dist * BETA
    p18 = power(scaled, 18.09)
    p08 = p18 * step_of(8.09, 18.09)
    first = keep(p18, dist, 0, 36)
    low = [first, keep(p08 * step_of(0.10, 8.09), dist, 0, 17)]
    high = [first, keep(p18 * step_of(35.09, 18.09), dist, 17, 36), keep(p08, dist, 0, 26),
            keep(power(scaled, 45.09), dist, 37, 63)]
    return jnp.concatenate(low, axis=1), jnp.concatenate(high, axis=1)


def encode_right(dist):
    scaled = dist * BETA
    p18 = power(scaled, 18.09)
    p08 = p18 * step_of(8.09, 18.09)
    low = [keep(p08 * step_of(0.10, 8.09), dist, 0, 17), keep(p18, dist, 18, 36)]
    high = [keep(power(scaled, 35.09), dist, 17, 53), keep(p18, dist, 0, 16),
            keep(power(scaled, 45.09), dist, 54, 63), keep(p08, dist, 0, 26)]
    return jnp.concatenate(low, axis=0), jnp.concatenate(high, axis=0)


def product(left, right):
    return jnp.dot(left, right, preferred_element_type=jnp.float32)


def decode(low, high):
    low = (LOW_SUM - SLACK) - jnp.log2(low) * (1.0 / BETA)
    high = (HIGH_SUM - SLACK) - jnp.log2(high) * (1.0 / BETA)
    return jnp.ceil(jnp.minimum(low, jnp.maximum(high, HIGH_FIRST)))


def min_plus(left, right):
    return decode(product(left[0], right[0]), product(left[1], right[1]))


def strips_kernel(offset, rows, cols, strip_rows, strip_cols):
    for part, strip in ((rows, strip_rows), (cols, strip_cols)):
        gap = lax.broadcasted_iota(jnp.int32, part.shape, 0) - lax.broadcasted_iota(jnp.int32, part.shape, 1)
        kept = jnp.where(gap == -offset[0], 0, part[...])
        strip[...] = kept.astype(jnp.float32).astype(jnp.bfloat16)


def strips(offset, weights):
    rows, cols = weights.shape
    corner = lambda shape: pl.BlockSpec(shape, lambda i: (0, 0))
    shapes = (PIVOT, cols), (rows, PIVOT)
    return pl.pallas_call(
        strips_kernel,
        out_shape=tuple(jax.ShapeDtypeStruct(shape, jnp.bfloat16) for shape in shapes),
        grid=(1,),
        in_specs=[pl.BlockSpec(memory_space=pltpu.SMEM)] + [corner(shape) for shape in shapes],
        out_specs=tuple(corner(shape) for shape in shapes),
    )(offset, weights, weights)


def close_block(block):
    def square(_, now):
        return jnp.minimum(now, min_plus(encode_left(now), encode_right(now)))

    return lax.fori_loop(0, 6, square, block)


def gather_close_kernel(n_row, n_col, strip_rows, strip_cols, panel_rows, closed,
                        panel_cols, pivots, dist, low_right, high_right,
                        send_piv, recv_piv, pass_piv, send_rows, recv_rows, pass_rows,
                        send_cols, recv_cols, local_sem):
    r, c = lax.axis_index("row"), lax.axis_index("col")
    row_gap, col_gap = n_row // STEPS, n_col // STEPS
    leader = lax.rem(r, row_gap) == 0
    group = r // row_gap
    rows_dev = strip_cols.shape[0]
    barrier = pltpu.get_barrier_semaphore()
    for k in range(1, n_row):
        pl.semaphore_signal(barrier, inc=1, device_id=(lax.rem(r + k, n_row), c), device_id_type=MESH)
    for k in range(1, n_col):
        pl.semaphore_signal(barrier, inc=1, device_id=(r, lax.rem(c + k, n_col)), device_id_type=MESH)
    pl.semaphore_wait(barrier, n_row + n_col - 2)

    parts = pl.ds(0, PIVOT), pl.ds(PIVOT, rows_dev - PIVOT)

    def cols_copy(s, part, k):
        return pltpu.make_async_remote_copy(
            src_ref=strip_cols.at[parts[part]], dst_ref=panel_cols.at[s, parts[part]],
            send_sem=send_cols.at[part, k - 1], recv_sem=recv_cols.at[part, s],
            device_id=(r, lax.rem(c + k, n_col)), device_id_type=MESH)

    def cols_own(s, part):
        return pltpu.make_async_copy(
            strip_cols.at[parts[part]], panel_cols.at[s, parts[part]], local_sem.at[part])

    def to_leader(src, dst, s, k, send, recv):
        return pltpu.make_async_remote_copy(
            src_ref=src, dst_ref=dst.at[s], send_sem=send.at[k - 1], recv_sem=recv.at[s],
            device_id=(lax.rem(r + k * row_gap, n_row), c), device_id_type=MESH)

    def to_member(src, dst, s, m, send, recv):
        return pltpu.make_async_remote_copy(
            src_ref=src, dst_ref=dst.at[s], send_sem=send.at[s, m - 1], recv_sem=recv.at[s],
            device_id=(r + m, c), device_id_type=MESH)

    corner = panel_cols.at[:, parts[0]]
    piv = pivots, send_piv, recv_piv
    row = panel_rows, send_rows, recv_rows

    for s in range(STEPS):
        @pl.when(c == s * col_gap)
        def _():
            @pl.when(leader)
            def _():
                for k in range(1, n_col):
                    cols_copy(s, 0, k).start()
            cols_own(s, 0).start()
            cols_own(s, 1).start()
            cols_own(s, 0).wait()
            cols_own(s, 1).wait()

    for s in range(STEPS):
        @pl.when(leader & (c != s * col_gap))
        def _():
            cols_copy(s, 0, 1).wait_recv()

    for s in range(STEPS):
        @pl.when(leader & (group == s))
        def _():
            for k in range(1, STEPS):
                to_leader(corner, pivots, s, k, send_piv, recv_piv).start()
            for m in range(1, row_gap):
                to_member(corner, pivots, s, m, pass_piv, recv_piv).start()
            for k in range(1, STEPS):
                to_leader(strip_rows, panel_rows, s, k, send_rows, recv_rows).start()
            for m in range(1, row_gap):
                to_member(strip_rows, panel_rows, s, m, pass_rows, recv_rows).start()
            own_piv = pltpu.make_async_copy(corner, pivots.at[s], local_sem.at[0])
            own_row = pltpu.make_async_copy(strip_rows, panel_rows.at[s], local_sem.at[1])
            own_piv.start()
            own_row.start()
            own_piv.wait()
            own_row.wait()

    for s in range(STEPS):
        @pl.when(leader & (c == s * col_gap))
        def _():
            for k in range(1, n_col):
                cols_copy(s, 1, k).start()

    def pass_on(dst, passing, send, recv):
        for j in range(1, STEPS):
            s = lax.rem(group + j, STEPS)

            @pl.when(leader)
            def _():
                to_leader(dst.at[0], dst, s, 1, send, recv).wait_recv()
                for m in range(1, row_gap):
                    to_member(dst.at[s], dst, s, m, passing, recv).start()

    pass_on(pivots, pass_piv, send_piv, recv_piv)

    @pl.when(jnp.logical_not(leader))
    def _():
        for s in range(STEPS):
            to_member(pivots.at[s], pivots, s, 1, pass_piv, recv_piv).wait_recv()

    for s in range(STEPS):
        @pl.when(jnp.logical_not(leader) & (c == s * col_gap))
        def _():
            for part in range(2):
                for k in range(1, n_col):
                    cols_copy(s, part, k).start()

    size = STEPS * PIVOT
    for s in range(STEPS):
        for t in range(STEPS):
            dist[s * PIVOT : (s + 1) * PIVOT, t * PIVOT : (t + 1) * PIVOT] = pivots[s, t].astype(jnp.float32)
    for s in range(STEPS):
        mine = slice(s * PIVOT, (s + 1) * PIVOT)
        block = close_block(dist[mine, mine])
        column = min_plus(encode_left(dist[:, mine]), encode_right(block))
        dist[...] = jnp.minimum(dist[...], min_plus(encode_left(column), encode_right(dist[mine, :])))
        if s == STEPS // 2 - 1:
            pass_on(panel_rows, pass_rows, send_rows, recv_rows)

    for s in range(STEPS):
        low, high = encode_right(dist[s * PIVOT : (s + 1) * PIVOT, :])
        low_right[s] = low
        high_right[s] = high

    for s in range(STEPS):
        @pl.when(c != s * col_gap)
        def _():
            cols_copy(s, 1, 1).wait_recv()

        @pl.when(jnp.logical_not(leader) & (c != s * col_gap))
        def _():
            cols_copy(s, 0, 1).wait_recv()

    tile = 256

    def update(index, carry):
        part = pl.ds(pl.multiple_of(index * tile, tile), tile)
        low = high = None
        for s in range(STEPS):
            left = encode_left(panel_cols[s, part, :].astype(jnp.float32))
            one, two = product(left[0], low_right[s]), product(left[1], high_right[s])
            low = one if s == 0 else jnp.maximum(low, one)
            high = two if s == 0 else jnp.maximum(high, two)
        best = jnp.minimum(decode(low, high), 64.0).astype(jnp.bfloat16)
        for s in range(STEPS):
            closed[s, part, :] = best[:, s * PIVOT : (s + 1) * PIVOT]
        return carry

    lax.fori_loop(0, rows_dev // tile, update, 0)

    @pl.when(jnp.logical_not(leader))
    def _():
        for s in range(STEPS):
            to_member(panel_rows.at[s], panel_rows, s, 1, pass_rows, recv_rows).wait_recv()

    for s in range(STEPS):
        @pl.when(c == s * col_gap)
        def _():
            for part in range(2):
                for k in range(1, n_col):
                    cols_copy(s, part, k).wait_send()

        @pl.when(leader)
        def _():
            for m in range(1, row_gap):
                to_member(pivots.at[s], pivots, s, m, pass_piv, recv_piv).wait_send()
                to_member(panel_rows.at[s], panel_rows, s, m, pass_rows, recv_rows).wait_send()

    @pl.when(leader)
    def _():
        for k in range(1, STEPS):
            to_leader(corner, pivots, 0, k, send_piv, recv_piv).wait_send()
            to_leader(strip_rows, panel_rows, 0, k, send_rows, recv_rows).wait_send()


def gather_close(n_row, n_col, strip_rows, strip_cols):
    rows_dev, cols_dev = strip_cols.shape[0], strip_rows.shape[1]
    vmem = pl.BlockSpec(memory_space=pltpu.VMEM)
    dma = pltpu.SemaphoreType.DMA
    size = STEPS * PIVOT
    members = max(n_row // STEPS - 1, 1)
    return pl.pallas_call(
        lambda *refs: gather_close_kernel(n_row, n_col, *refs),
        out_shape=(
            jax.ShapeDtypeStruct((STEPS, PIVOT, cols_dev), jnp.bfloat16),
            jax.ShapeDtypeStruct((STEPS, rows_dev, PIVOT), jnp.bfloat16),
        ),
        in_specs=[vmem] * 2,
        out_specs=(vmem,) * 2,
        scratch_shapes=[
            pltpu.VMEM((STEPS, rows_dev, PIVOT), jnp.bfloat16),
            pltpu.VMEM((STEPS, STEPS, PIVOT, PIVOT), jnp.bfloat16),
            pltpu.VMEM((size, size), jnp.float32),
            pltpu.VMEM((STEPS, 2 * PIVOT, size), jnp.bfloat16),
            pltpu.VMEM((STEPS, 4 * PIVOT, size), jnp.bfloat16),
            dma((STEPS - 1,)), dma((STEPS,)), dma((STEPS, members)),
            dma((STEPS - 1,)), dma((STEPS,)), dma((STEPS, members)),
            dma((2, n_col - 1)), dma((2, STEPS)), dma((2,)),
        ],
        compiler_params=pltpu.CompilerParams(collective_id=0, has_side_effects=True),
    )(strip_rows, strip_cols)


def finish_kernel(offset, closed, panel_rows, weights, out, low_right, high_right, low_left, high_left):
    tile, cols = weights.shape
    wide = 256

    @pl.when(pl.program_id(0) == 0)
    def _():
        def one(index, carry):
            s, part = index // (cols // wide), index % (cols // wide)
            where = pl.ds(pl.multiple_of(part * wide, wide), wide)
            low, high = encode_right(panel_rows[s, :, where].astype(jnp.float32))
            low_right[s, :, where] = low
            high_right[s, :, where] = high
            return carry

        lax.fori_loop(0, STEPS * (cols // wide), one, 0)

    for s in range(STEPS):
        low, high = encode_left(closed[s].astype(jnp.float32))
        low_left[s] = low
        high_left[s] = high

    base = offset[0] + pl.program_id(0) * tile

    def columns(index, carry):
        start = pl.multiple_of(index * wide, wide)
        where = pl.ds(start, wide)
        low = product(low_left[0], low_right[0, :, where])
        high = product(high_left[0], high_right[0, :, where])
        for s in range(1, STEPS):
            low = jnp.maximum(low, product(low_left[s], low_right[s, :, where]))
            high = jnp.maximum(high, product(high_left[s], high_right[s, :, where]))
        shape = (tile, wide)
        gap = lax.broadcasted_iota(jnp.int32, shape, 0) - lax.broadcasted_iota(jnp.int32, shape, 1)
        old = jnp.where(gap == start - base, 0, weights[:, where])
        best = jnp.minimum(decode(low, high), 64.0).astype(jnp.int32)
        out[:, where] = jnp.minimum(old, best)
        return carry

    lax.fori_loop(0, cols // wide, columns, 0)


def finish(offset, closed, panel_rows, weights):
    rows, cols = weights.shape
    tile = 256
    return pl.pallas_call(
        finish_kernel,
        out_shape=jax.ShapeDtypeStruct(weights.shape, jnp.int32),
        grid=(rows // tile,),
        in_specs=[
            pl.BlockSpec(memory_space=pltpu.SMEM),
            pl.BlockSpec((STEPS, tile, PIVOT), lambda i: (0, i, 0)),
            pl.BlockSpec((STEPS, PIVOT, cols), lambda i: (0, 0, 0)),
            pl.BlockSpec((tile, cols), lambda i: (i, 0)),
        ],
        out_specs=pl.BlockSpec((tile, cols), lambda i: (i, 0)),
        scratch_shapes=[
            pltpu.VMEM((STEPS, 2 * PIVOT, cols), jnp.bfloat16),
            pltpu.VMEM((STEPS, 4 * PIVOT, cols), jnp.bfloat16),
            pltpu.VMEM((STEPS, tile, 2 * PIVOT), jnp.bfloat16),
            pltpu.VMEM((STEPS, tile, 4 * PIVOT), jnp.bfloat16),
        ],
    )(offset, closed, panel_rows, weights)


def solution(mesh):
    n_row, n_col = mesh.shape["row"], mesh.shape["col"]
    assert n_row % STEPS == 0 and n_col % STEPS == 0

    def per_device(weights):
        rows_dev, cols_dev = weights.shape
        offset = lax.axis_index("row") * rows_dev - lax.axis_index("col") * cols_dev
        offset = jnp.full((1,), offset, jnp.int32)
        panel_rows, closed = gather_close(n_row, n_col, *strips(offset, weights))
        return finish(offset, closed, panel_rows, weights)

    return jax.shard_map(
        per_device, mesh=mesh, in_specs=(P("row", "col"),), out_specs=P("row", "col"), check_vma=False)
```

time: 65.3 us -> 46.7 us (0.72)
  Pallas kernels: 61.4 us -> 46.5 us
  other arithmetic: 3.65 us -> 0 us
    pallas_call x2, Pallas kernels: 49.4 us -> 34.9 us  [the longest x1 33 us: gather_close(): pl.pallas_call(lambda *refs: gather_close_kernel(n_row, n_col, *refs), ou...]
    convert_element_type x2 -> x0, other arithmetic: 3.64 us -> none  [strip(): jnp.where(down[:height] == across[:, :width], 0, kept).astype(jnp.bfloat16)]
where the time goes in v2:
time: 46.7 us; the launch traced here: 46.6 us
  Pallas kernels  46.5 us (100%)
    pallas_call x1, Pallas kernels, gather_close(): pl.pallas_call(lambda *refs: gather_close_kernel(n_row, n_col, *refs), ou...  33 us
    pallas_call x1, Pallas kernels, finish(): pl.pallas_call(finish_kernel, out_shape=jax.ShapeDtypeStruct(weights.shap...  11.6 us
    pallas_call x1, Pallas kernels, strips(): pl.pallas_call(strips_kernel, out_shape=tuple((jax.ShapeDtypeStruct(shape...  1.93 us

profile of v2, /device:TPU:1, one launch (start us, length us, event | category | flops | bytes accessed | tf_op | source)
XLA Modules:
  0.0 46.6 jit_solution(10511750298453879878)
XLA Ops:
  0.0 1.9 %shard_map.17 = (bf16[128,1024]{1,0:T(8,128)(2,1)}, bf16[512,128]{1,0:T(8,128)(2,1)}) custom-call(s32[1]{0:T(128)} %bitcast.offset, s32[512,1024]{1,0:T(8,128)} %weights.1, s32[512,1024]{1,0:T(8,128)} %weights.1), custom_call_target="tpu_custom_call" | custom-call | tf_op jit(solution)/shard_map/pallas_call | solution.py:80
  1.9 33.0 %shard_map.18 = (bf16[4,128,1024]{2,1,0:T(8,128)(2,1)}, bf16[4,512,128]{2,1,0:T(8,128)(2,1)}) custom-call(bf16[128,1024]{1,0:T(8,128)(2,1)} %get-tuple-element.9.refs_0_, bf16[512,128]{1,0:T(8,128)(2,1)} %get-tuple-element.10.refs_1_), custom_call_target="tpu_custom_call" | custom-call | tf_op jit(solution)/shard_map/pallas_call | solution.py:277
  34.9 11.6 %shard_map.19 = s32[512,1024]{1,0:T(8,128)} custom-call(s32[1]{0:T(128)} %bitcast.offset, bf16[4,512,128]{2,1,0:T(8,128)(2,1)} %get-tuple-element.11.closed, bf16[4,128,1024]{2,1,0:T(8,128)(2,1)} %get-tuple-element.12.panel_rows, s32[512,1024]{1,0:T(8,128)} %weights.1), custom_call_target="tpu_custom_call" | custom-call | tf_op jit(solution)/shard_map/pallas_call | solution.py:343

commit v3 on v2

--- a/solution.py
+++ b/solution.py
@@ -27,8 +27,9 @@
 
 
 def keep(value, dist, first, last):
+    dist = dist.astype(jnp.bfloat16)
     kept = dist <= last if first == 0 else (dist >= first) & (dist <= last)
-    return jnp.where(kept, value, 0.0).astype(jnp.bfloat16)
+    return jnp.where(kept, value.astype(jnp.bfloat16), jnp.bfloat16(0))
 
 
 def encode_left(dist):

time: 46.7 us -> 45.2 us (0.968)
  Pallas kernels: 46.5 us -> 45 us
    pallas_call x1, Pallas kernels: 33 us -> 32.1 us  [gather_close(): pl.pallas_call(lambda *refs: gather_close_kernel(n_row, n_col, *refs), ou...]
    pallas_call x1, Pallas kernels: 11.6 us -> 11 us  [finish(): pl.pallas_call(finish_kernel, out_shape=jax.ShapeDtypeStruct(weights.shap...]
where the time goes in v3:
time: 45.2 us; the launch traced here: 45 us
  Pallas kernels  45 us (100%)
    pallas_call x1, Pallas kernels, gather_close(): pl.pallas_call(lambda *refs: gather_close_kernel(n_row, n_col, *refs), ou...  32.1 us
    pallas_call x1, Pallas kernels, finish(): pl.pallas_call(finish_kernel, out_shape=jax.ShapeDtypeStruct(weights.shap...  11 us
    pallas_call x1, Pallas kernels, strips(): pl.pallas_call(strips_kernel, out_shape=tuple((jax.ShapeDtypeStruct(shape...  1.93 us

profile of v3, /device:TPU:1, one launch (start us, length us, event | category | flops | bytes accessed | tf_op | source)
XLA Modules:
  0.0 45.0 jit_solution(10447688746879577661)
XLA Ops:
  0.0 1.9 %shard_map.17 = (bf16[128,1024]{1,0:T(8,128)(2,1)}, bf16[512,128]{1,0:T(8,128)(2,1)}) custom-call(s32[1]{0:T(128)} %bitcast.offset, s32[512,1024]{1,0:T(8,128)} %weights.1, s32[512,1024]{1,0:T(8,128)} %weights.1), custom_call_target="tpu_custom_call" | custom-call | tf_op jit(solution)/shard_map/pallas_call | solution.py:81
  1.9 32.1 %shard_map.18 = (bf16[4,128,1024]{2,1,0:T(8,128)(2,1)}, bf16[4,512,128]{2,1,0:T(8,128)(2,1)}) custom-call(bf16[128,1024]{1,0:T(8,128)(2,1)} %get-tuple-element.9.refs_0_, bf16[512,128]{1,0:T(8,128)(2,1)} %get-tuple-element.10.refs_1_), custom_call_target="tpu_custom_call" | custom-call | tf_op jit(solution)/shard_map/pallas_call | solution.py:278
  34.0 11.0 %shard_map.19 = s32[512,1024]{1,0:T(8,128)} custom-call(s32[1]{0:T(128)} %bitcast.offset, bf16[4,512,128]{2,1,0:T(8,128)(2,1)} %get-tuple-element.11.closed, bf16[4,128,1024]{2,1,0:T(8,128)(2,1)} %get-tuple-element.12.panel_rows, s32[512,1024]{1,0:T(8,128)} %weights.1), custom_call_target="tpu_custom_call" | custom-call | tf_op jit(solution)/shard_map/pallas_call | solution.py:344

commit v4 on v3

--- a/solution.py
+++ b/solution.py
@@ -242,7 +242,7 @@
             closed[s, part, :] = best[:, s * PIVOT : (s + 1) * PIVOT]
         return carry
 
-    lax.fori_loop(0, rows_dev // tile, update, 0)
+    lax.fori_loop(0, rows_dev // tile, update, 0, unroll=True)
 
     @pl.when(jnp.logical_not(leader))
     def _():
@@ -311,7 +311,7 @@
             high_right[s, :, where] = high
             return carry
 
-        lax.fori_loop(0, STEPS * (cols // wide), one, 0)
+        lax.fori_loop(0, STEPS * (cols // wide), one, 0, unroll=2)
 
     for s in range(STEPS):
         low, high = encode_left(closed[s].astype(jnp.float32))
@@ -335,7 +335,7 @@
         out[:, where] = jnp.minimum(old, best)
         return carry
 
-    lax.fori_loop(0, cols // wide, columns, 0)
+    lax.fori_loop(0, cols // wide, columns, 0, unroll=2)
 
 
 def finish(offset, closed, panel_rows, weights):

time: 45.2 us -> 44.6 us (0.987)
  Pallas kernels: 45 us -> 44.5 us
where the time goes in v4:
time: 44.6 us; the launch traced here: 44.5 us
  Pallas kernels  44.5 us (100%)
    pallas_call x1, Pallas kernels, gather_close(): pl.pallas_call(lambda *refs: gather_close_kernel(n_row, n_col, *refs), ou...  31.8 us
    pallas_call x1, Pallas kernels, finish(): pl.pallas_call(finish_kernel, out_shape=jax.ShapeDtypeStruct(weights.shap...  10.8 us
    pallas_call x1, Pallas kernels, strips(): pl.pallas_call(strips_kernel, out_shape=tuple((jax.ShapeDtypeStruct(shape...  1.93 us

profile of v4, /device:TPU:1, one launch (start us, length us, event | category | flops | bytes accessed | tf_op | source)
XLA Modules:
  0.0 44.5 jit_solution(12874206645589073229)
XLA Ops:
  0.0 1.9 %shard_map.17 = (bf16[128,1024]{1,0:T(8,128)(2,1)}, bf16[512,128]{1,0:T(8,128)(2,1)}) custom-call(s32[1]{0:T(128)} %bitcast.offset, s32[512,1024]{1,0:T(8,128)} %weights.1, s32[512,1024]{1,0:T(8,128)} %weights.1), custom_call_target="tpu_custom_call" | custom-call | tf_op jit(solution)/shard_map/pallas_call | solution.py:81
  1.9 31.8 %shard_map.18 = (bf16[4,128,1024]{2,1,0:T(8,128)(2,1)}, bf16[4,512,128]{2,1,0:T(8,128)(2,1)}) custom-call(bf16[128,1024]{1,0:T(8,128)(2,1)} %get-tuple-element.9.refs_0_, bf16[512,128]{1,0:T(8,128)(2,1)} %get-tuple-element.10.refs_1_), custom_call_target="tpu_custom_call" | custom-call | tf_op jit(solution)/shard_map/pallas_call | solution.py:278
  33.7 10.8 %shard_map.19 = s32[512,1024]{1,0:T(8,128)} custom-call(s32[1]{0:T(128)} %bitcast.offset, bf16[4,512,128]{2,1,0:T(8,128)(2,1)} %get-tuple-element.11.closed, bf16[4,128,1024]{2,1,0:T(8,128)(2,1)} %get-tuple-element.12.panel_rows, s32[512,1024]{1,0:T(8,128)} %weights.1), custom_call_target="tpu_custom_call" | custom-call | tf_op jit(solution)/shard_map/pallas_call | solution.py:344
